TPU v7x, 32 devices: a whole 2x2x4 slice. The times are simulated.
32 devices in a mesh: slab: 8 (over y, x, core), det: 4 (over z).
Axes of the slice: x: 2, y: 2, z: 4, core: 2. Of those that a mesh axis runs over, the one named last changes fastest.
Arguments:
- traces: float32 [32, 128, 4096], P(('slab', 'det')), may hold values from -6 to 6
- tables: bfloat16 [32, 256, 2048], P('slab', None, 'det'), may hold values from -0.0625 to 0.0625
- slab_range: int32 [32, 2], P(('slab', 'det')), may hold values from 0 to 7, as said below
- table_slot: int32 [32, 7], P(('slab', 'det')), may hold values from 0 to 3
- sample_start: int32 [32, 7], P(('slab', 'det')), may hold values from 0 to 3840
Outputs:
- image: float32 [128, 16384], P(None, ('slab', 'det'))
Inputs may be any that keep to these rules, and one draw needn't show every extreme that they name: For detector d with home slab g = d // 4: max(0, g - 3) <= slab_range[d, 0] <= g <= slab_range[d, 1] <= min(7, g + 3); some detectors reach the full 3 on both sides where the grid allows.
All inputs are finite; a program needn't handle non-finite values.
Results may differ from a plain program's by a relative error of at most 0.007.
Values may be sent and summed in bfloat16 or wider, within the bound.
No kernel may reach another device: no remote copies, remote signals or barrier semaphores. Data moves between devices by JAX's collectives and lax.ppermute only.
A program may use at most 64 MiB of HBM per device.

v0:
```python
import jax
import jax.numpy as jnp
from jax import lax
from jax.sharding import PartitionSpec as P

KWIN = 256
NTAB = 4
RANGE = 3


def shifted(x, axis, by):
    peers = lax.axis_size(axis)
    pairs = [(i, i + by) for i in range(peers) if 0 <= i + by < peers]
    return lax.ppermute(x, axis, pairs)


def cut_windows(trace_rows, starts):

    def single(trace_row, first_index):
        return lax.dynamic_slice_in_dim(trace_row, first_index, KWIN, 1)

    return jax.vmap(single)(trace_rows, starts)


def bin_windows(windows, slot_ids, active):
    onehot = (slot_ids[:, None] == jnp.arange(NTAB, dtype=jnp.int32)[None, :]) & active[:, None]
    onehot = onehot.astype(jnp.bfloat16)
    return jnp.einsum("it,ifk->tfk", onehot, windows, preferred_element_type=jnp.float32)


def body(traces, tables, slab_range, table_slot, sample_start):
    position = lax.axis_index("slab")
    samples = traces.astype(jnp.bfloat16)
    own_active = (slab_range[:, 0] <= position) & (position <= slab_range[:, 1])
    stacked = bin_windows(
        cut_windows(samples, sample_start[:, RANGE]), table_slot[:, RANGE], own_active
    )
    for offset in list(range(-RANGE, 0)) + list(range(1, RANGE + 1)):
        target = position + offset
        active = (slab_range[:, 0] <= target) & (target <= slab_range[:, 1])
        windows = cut_windows(samples, sample_start[:, offset + RANGE])
        windows = windows * active[:, None, None].astype(jnp.bfloat16)
        arrived_windows, arrived_slots = shifted(
            (windows, table_slot[:, offset + RANGE]), "slab", offset
        )
        everything = jnp.ones(arrived_slots.shape, jnp.bool_)
        stacked = stacked + bin_windows(arrived_windows, arrived_slots, everything)
    binned = stacked.astype(jnp.bfloat16)
    partial_image = jnp.einsum(
        "tfk,tkv->fv",
        binned,
        lax.all_gather(tables, "det", axis=2, tiled=True),
        preferred_element_type=jnp.float32,
    )
    return lax.psum_scatter(partial_image, "det", scatter_dimension=1, tiled=True)


def solution(mesh):
    placed = (
        P(("slab", "det"), None, None),
        P("slab", None, "det"),
        P(("slab", "det"), None),
        P(("slab", "det"), None),
        P(("slab", "det"), None),
    )
    return jax.shard_map(
        body, mesh=mesh, in_specs=placed, out_specs=P(None, ("slab", "det")), check_vma=False
    )
```

profile of v0, /device:TPU:0, one launch (start us, length us, event | category | flops | bytes accessed | tf_op | source)
XLA Modules:
  0.0 129.3 jit_solution(1520195266104620349)
XLA Ops:
  6.5 0.0 all-gather.2.cloned.1.call-start
  6.5 0.7 all-gather.2.cloned.1.call-update
  7.3 0.0 reduce-scatter.2.cloned.1.call-start
  7.3 1.6 %fusion.21 = (s32[1,1]{1,0:T(1,128)}, s32[1,1]{1,0:T(1,128)}, s32[1,1]{1,0:T(1,128)}, s32[1,1]{1,0:T(1,128)}, s32[1,1]{1,0:T(1,128)}, /*index=5*/s32[1,1]{1,0:T(1,128)}, s32[1,1]{1,0:T(1,128)}) fusion(s32[1,7]{1,0:T(1,128)} %param.8), kind=kLoop, calls=%fused_computation.43 | loop fusion | bytes 56 | tf_op jit(solution)/shard_map/slice | solution.py:36
  8.9 3.0 %collective-permute-start.6 = (s32[1]{0:T(128)}, s32[1]{0:T(128)}, u32[]{:S(2)}, u32[]{:S(2)}) collective-permute-start(s32[1]{0:T(128)} %bitcast.33), channel_id=1, source_target_pairs={{0,4},{4,8},{8,12},{12,16},{16,20},{20,24},{24,28},{1,5},{5,9},{9,... | collective-permute-start | bytes 20 | tf_op jit(solution)/shard_map/ppermute | solution.py:14
  11.9 1.3 collective-permute-start.4
  13.1 1.3 collective-permute-start.2
  14.4 1.3 collective-permute-start
  15.7 7.7 %collective-permute-start.10 = (s32[1]{0:T(128)}, s32[1]{0:T(128)}, u32[]{:S(2)}, u32[]{:S(2)}) collective-permute-start(s32[1]{0:T(128)} %bitcast.49), channel_id=1, source_target_pairs={{0,12},{4,16},{8,20},{12,24},{16,28},{1,13},{5,17},{9,21},{13,25},... | collective-permute-start | bytes 20 | tf_op jit(solution)/shard_map/ppermute | solution.py:14
  23.4 1.3 %fusion.23 = (s32[1,1]{1,0:T(1,128)}, s32[1,1]{1,0:T(1,128)}) fusion(s32[1,2]{1,0:T(1,128)} %param.7), kind=kLoop, calls=%fused_computation.45 | loop fusion | bytes 16 | tf_op jit(solution)/shard_map/slice | solution.py:34
  33.7 1.6 %fusion.22 = (s32[1,1]{1,0:T(1,128)}, s32[1,1]{1,0:T(1,128)}, s32[1,1]{1,0:T(1,128)}, s32[1,1]{1,0:T(1,128)}, s32[1,1]{1,0:T(1,128)}, /*index=5*/s32[1,1]{1,0:T(1,128)}, s32[1,1]{1,0:T(1,128)}) fusion(s32[1,7]{1,0:T(1,128)} %param.9), kind=kLoop, calls=%fused_computation.44 | loop fusion | bytes 56 | tf_op jit(solution)/shard_map/slice | solution.py:36
  44.2 1.7 %convert_element_type.10 = bf16[1,128,4096]{2,1,0:T(8,128)(2,1)S(1)} convert(f32[1,128,4096]{2,1,0:T(8,128)} %param.5) | non-fusion elementwise | flops 524288 | bytes 3145728 | tf_op jit(solution)/shard_map/convert_element_type | solution.py:33
  50.4 0.6 fusion.14
  51.0 0.2 bitcast_convert_fusion.6
  51.2 0.0 collective-permute-done.6
  51.2 5.9 %collective-permute-start.8 = (s32[1]{0:T(128)}, s32[1]{0:T(128)}, u32[]{:S(2)}, u32[]{:S(2)}) collective-permute-start(s32[1]{0:T(128)} %bitcast.41), channel_id=1, source_target_pairs={{0,8},{4,12},{8,16},{12,20},{16,24},{20,28},{1,9},{5,13},{9,17},{1... | collective-permute-start | bytes 20 | tf_op jit(solution)/shard_map/ppermute | solution.py:14
  57.1 0.7 fusion.18
  57.8 0.0 collective-permute-done.4
  57.8 1.3 %collective-permute-start.11 = (bf16[1,128,256]{2,1,0:T(8,128)(2,1)S(1)}, bf16[1,128,256]{2,1,0:T(8,128)(2,1)S(1)}, u32[]{:S(2)}, u32[]{:S(2)}) collective-permute-start(bf16[1,128,256]{2,1,0:T(8,128)(2,1)S(1)} %get-tuple-element.83), channel_id=1, source_target_pairs={{0,12},{4,16},{8,20},{12,24},{16,28},{1,13},{5,17},{9,21},{13,25},... | collective-permute-start | bytes 196616 | tf_op jit(solution)/shard_map/ppermute | solution.py:14
  59.1 0.6 fusion.17
  59.8 0.0 collective-permute-done.2
  59.8 2.9 %collective-permute-start.9 = (bf16[1,128,256]{2,1,0:T(8,128)(2,1)S(1)}, bf16[1,128,256]{2,1,0:T(8,128)(2,1)S(1)}, u32[]{:S(2)}, u32[]{:S(2)}) collective-permute-start(bf16[1,128,256]{2,1,0:T(8,128)(2,1)S(1)} %get-tuple-element.84), channel_id=1, source_target_pairs={{0,8},{4,12},{8,16},{12,20},{16,24},{20,28},{1,9},{5,13},{9,17},{1... | collective-permute-start | bytes 196616 | tf_op jit(solution)/shard_map/ppermute | solution.py:14
  62.6 0.6 fusion.16
  63.3 0.0 collective-permute-done
  63.3 1.3 %collective-permute-start.7 = (bf16[1,128,256]{2,1,0:T(8,128)(2,1)S(1)}, bf16[1,128,256]{2,1,0:T(8,128)(2,1)S(1)}, u32[]{:S(2)}, u32[]{:S(2)}) collective-permute-start(bf16[1,128,256]{2,1,0:T(8,128)(2,1)S(1)} %get-tuple-element.85), channel_id=1, source_target_pairs={{0,4},{4,8},{8,12},{12,16},{16,20},{20,24},{24,28},{1,5},{5,9},{9,... | collective-permute-start | bytes 196616 | tf_op jit(solution)/shard_map/ppermute | solution.py:14
  64.6 0.6 fusion.15
  65.2 0.0 collective-permute-done.10
  65.3 1.3 collective-permute-start.5
  66.6 0.6 fusion.20
  67.2 0.0 collective-permute-done.8
  67.2 1.3 collective-permute-start.3
  68.5 0.7 fusion.19
  69.2 0.0 collective-permute-done.11
  69.2 1.3 collective-permute-start.1
  70.5 0.0 collective-permute-done.9
  70.5 0.0 collective-permute-done.7
  70.6 0.0 collective-permute-done.5
  70.6 4.5 %collective-permute-done.3 = bf16[1,128,256]{2,1,0:T(8,128)(2,1)S(1)} collective-permute-done((bf16[1,128,256]{2,1,0:T(8,128)(2,1)S(1)}, bf16[1,128,256]{2,1,0:T(8,128)(2,1)S(1)}, u32[]{:S(2)}, u32[]{:S(2)}) %collective-permute-start.3) | collective-permute-done | bytes 65568 | tf_op jit(solution)/shard_map/ppermute | solution.py:14
  75.1 1.9 %collective-permute-done.1 = bf16[1,128,256]{2,1,0:T(8,128)(2,1)S(1)} collective-permute-done((bf16[1,128,256]{2,1,0:T(8,128)(2,1)S(1)}, bf16[1,128,256]{2,1,0:T(8,128)(2,1)S(1)}, u32[]{:S(2)}, u32[]{:S(2)}) %collective-permute-start.1) | collective-permute-done | bytes 65568 | tf_op jit(solution)/shard_map/ppermute | solution.py:14
  77.0 15.4 %all-gather.2.cloned.1.call-done = bf16[4,256,2048]{2,1,0:T(8,128)(2,1)} async-done(((bf16[4,256,512]{2,1,0:T(8,128)(2,1)}), bf16[4,256,2048]{2,1,0:T(8,128)(2,1)}) %all-gather.2.cloned.1.call-update) | async-done | bytes 4194320 | tf_op jit(solution)/shard_map/all_gather | solution.py:52
  92.4 4.1 %convolution_bitcast_fusion = f32[128,2048]{1,0:T(8,128)} fusion(bf16[4,256,2048]{2,1,0:T(8,128)(2,1)} %all-gather.2.cloned.1.call-done, f32[128,256]{1,0:T(8,128)S(1)} %bitcast_convert_fusion, f32[4]{0:T(128)S(1)} %fusion.20, f32[128,256]{1,0:T(8,128)S(1)} %bitcast_convert_fusion.1, f32[4]{0:T(128)S(1)} %fusion.19, f32[128,256]{1,0:T(8,128)S(1)} %bitcast_convert_fusion.2, ...), kind=kOutput, calls=%fused_computation | convolution fusion | flops 538705920 | bytes 6160496 | tf_op jit(solution)/shard_map/tfk,tkv->fv/dot_general | solution.py:49
  96.5 0.0 reduce-scatter.2.cloned.1.call-update
  96.5 25.9 %reduce-scatter.2.cloned.1.call-done = f32[128,512]{1,0:T(8,128)} async-done(((f32[128,2048]{1,0:T(8,128)}), f32[128,512]{1,0:T(8,128)}) %reduce-scatter.2.cloned.1.call-update) | async-done | bytes 262160 | tf_op jit(solution)/shard_map/reduce_scatter | solution.py:55
  (6 shorter events, 0.1 us)
Async XLA Ops:
  6.5 85.9 %all-gather.2.cloned.1.call-start = ((), (), s32[]{:S(2)}) async-start(), calls=%async_computation.1 | async-start | bytes 5242880 | tf_op jit(solution)/shard_map/all_gather | solution.py:52
  7.3 115.2 %reduce-scatter.2.cloned.1.call-start = ((), (), s32[]{:S(2)}) async-start(), calls=%async_computation.2 | async-start | bytes 1310720 | tf_op jit(solution)/shard_map/reduce_scatter | solution.py:55
  8.9 42.3 %collective-permute-start.6 = (s32[1]{0:T(128)}, s32[1]{0:T(128)}, u32[]{:S(2)}, u32[]{:S(2)}) collective-permute-start(s32[1]{0:T(128)} %bitcast.33), channel_id=1, source_target_pairs={{0,4},{4,8},{8,12},{12,16},{16,20},{20,24},{24,28},{1,5},{5,9},{9,... | collective-permute-start | bytes 20 | tf_op jit(solution)/shard_map/ppermute | solution.py:14
  11.9 46.0 %collective-permute-start.4 = (s32[1]{0:T(128)}, s32[1]{0:T(128)}, u32[]{:S(2)}, u32[]{:S(2)}) collective-permute-start(s32[1]{0:T(128)} %bitcast.25), channel_id=1, source_target_pairs={{4,0},{8,4},{12,8},{16,12},{20,16},{24,20},{28,24},{5,1},{9,5},{13... | collective-permute-start | bytes 20 | tf_op jit(solution)/shard_map/ppermute | solution.py:14
  13.1 46.6 %collective-permute-start.2 = (s32[1]{0:T(128)}, s32[1]{0:T(128)}, u32[]{:S(2)}, u32[]{:S(2)}) collective-permute-start(s32[1]{0:T(128)} %bitcast.17), channel_id=1, source_target_pairs={{8,0},{12,4},{16,8},{20,12},{24,16},{28,20},{9,1},{13,5},{17,9},{2... | collective-permute-start | bytes 20 | tf_op jit(solution)/shard_map/ppermute | solution.py:14
  14.4 48.8 %collective-permute-start = (s32[1]{0:T(128)}, s32[1]{0:T(128)}, u32[]{:S(2)}, u32[]{:S(2)}) collective-permute-start(s32[1]{0:T(128)} %bitcast.9), channel_id=1, source_target_pairs={{12,0},{16,4},{20,8},{24,12},{28,16},{13,1},{17,5},{21,9},{25,13},... | collective-permute-start | bytes 20 | tf_op jit(solution)/shard_map/ppermute | solution.py:14
  15.7 49.5 %collective-permute-start.10 = (s32[1]{0:T(128)}, s32[1]{0:T(128)}, u32[]{:S(2)}, u32[]{:S(2)}) collective-permute-start(s32[1]{0:T(128)} %bitcast.49), channel_id=1, source_target_pairs={{0,12},{4,16},{8,20},{12,24},{16,28},{1,13},{5,17},{9,21},{13,25},... | collective-permute-start | bytes 20 | tf_op jit(solution)/shard_map/ppermute | solution.py:14
  51.2 16.0 %collective-permute-start.8 = (s32[1]{0:T(128)}, s32[1]{0:T(128)}, u32[]{:S(2)}, u32[]{:S(2)}) collective-permute-start(s32[1]{0:T(128)} %bitcast.41), channel_id=1, source_target_pairs={{0,8},{4,12},{8,16},{12,20},{16,24},{20,28},{1,9},{5,13},{9,17},{1... | collective-permute-start | bytes 20 | tf_op jit(solution)/shard_map/ppermute | solution.py:14
  57.8 11.4 %collective-permute-start.11 = (bf16[1,128,256]{2,1,0:T(8,128)(2,1)S(1)}, bf16[1,128,256]{2,1,0:T(8,128)(2,1)S(1)}, u32[]{:S(2)}, u32[]{:S(2)}) collective-permute-start(bf16[1,128,256]{2,1,0:T(8,128)(2,1)S(1)} %get-tuple-element.83), channel_id=1, source_target_pairs={{0,12},{4,16},{8,20},{12,24},{16,28},{1,13},{5,17},{9,21},{13,25},... | collective-permute-start | bytes 196616 | tf_op jit(solution)/shard_map/ppermute | solution.py:14
  59.8 10.7 %collective-permute-start.9 = (bf16[1,128,256]{2,1,0:T(8,128)(2,1)S(1)}, bf16[1,128,256]{2,1,0:T(8,128)(2,1)S(1)}, u32[]{:S(2)}, u32[]{:S(2)}) collective-permute-start(bf16[1,128,256]{2,1,0:T(8,128)(2,1)S(1)} %get-tuple-element.84), channel_id=1, source_target_pairs={{0,8},{4,12},{8,16},{12,20},{16,24},{20,28},{1,9},{5,13},{9,17},{1... | collective-permute-start | bytes 196616 | tf_op jit(solution)/shard_map/ppermute | solution.py:14
  63.3 7.2 %collective-permute-start.7 = (bf16[1,128,256]{2,1,0:T(8,128)(2,1)S(1)}, bf16[1,128,256]{2,1,0:T(8,128)(2,1)S(1)}, u32[]{:S(2)}, u32[]{:S(2)}) collective-permute-start(bf16[1,128,256]{2,1,0:T(8,128)(2,1)S(1)} %get-tuple-element.85), channel_id=1, source_target_pairs={{0,4},{4,8},{8,12},{12,16},{16,20},{20,24},{24,28},{1,5},{5,9},{9,... | collective-permute-start | bytes 196616 | tf_op jit(solution)/shard_map/ppermute | solution.py:14
  65.3 5.3 %collective-permute-start.5 = (bf16[1,128,256]{2,1,0:T(8,128)(2,1)S(1)}, bf16[1,128,256]{2,1,0:T(8,128)(2,1)S(1)}, u32[]{:S(2)}, u32[]{:S(2)}) collective-permute-start(bf16[1,128,256]{2,1,0:T(8,128)(2,1)S(1)} %get-tuple-element.86), channel_id=1, source_target_pairs={{4,0},{8,4},{12,8},{16,12},{20,16},{24,20},{28,24},{5,1},{9,5},{13... | collective-permute-start | bytes 196616 | tf_op jit(solution)/shard_map/ppermute | solution.py:14
  67.2 7.9 %collective-permute-start.3 = (bf16[1,128,256]{2,1,0:T(8,128)(2,1)S(1)}, bf16[1,128,256]{2,1,0:T(8,128)(2,1)S(1)}, u32[]{:S(2)}, u32[]{:S(2)}) collective-permute-start(bf16[1,128,256]{2,1,0:T(8,128)(2,1)S(1)} %get-tuple-element.87), channel_id=1, source_target_pairs={{8,0},{12,4},{16,8},{20,12},{24,16},{28,20},{9,1},{13,5},{17,9},{2... | collective-permute-start | bytes 196616 | tf_op jit(solution)/shard_map/ppermute | solution.py:14
  69.2 7.8 %collective-permute-start.1 = (bf16[1,128,256]{2,1,0:T(8,128)(2,1)S(1)}, bf16[1,128,256]{2,1,0:T(8,128)(2,1)S(1)}, u32[]{:S(2)}, u32[]{:S(2)}) collective-permute-start(bf16[1,128,256]{2,1,0:T(8,128)(2,1)S(1)} %get-tuple-element.88), channel_id=1, source_target_pairs={{12,0},{16,4},{20,8},{24,12},{28,16},{13,1},{17,5},{21,9},{25,13},... | collective-permute-start | bytes 196616 | tf_op jit(solution)/shard_map/ppermute | solution.py:14
Sparse Core Ops, SparseCore 0:
  8.9 83.4 all-gather.1
  96.6 25.7 reduce-scatter.1
where the time goes:
time: 130 us; the launch traced here: 129 us
  waiting for transfers between devices  48.5 us (37%)
  between operations  36 us (28%)
  starting transfers between devices  29.8 us (23%)
  other arithmetic  6.48 us (5%)
  local copies, waits for them, and re-layouts  4.5 us (3%)
  matrix products  4.07 us (3%)
    ppermute x12, starting transfers between devices, shifted(): return lax.ppermute(x, axis, pairs)  29.8 us
    reduce_scatter x1, waiting for transfers between devices, body(): lax.psum_scatter(partial_image, 'det', scatter_dimension=1, tiled=True)  25.9 us
    all_gather x1, waiting for transfers between devices, body(): lax.all_gather(tables, 'det', axis=2, tiled=True)  15.4 us
    ppermute x12, waiting for transfers between devices, shifted(): return lax.ppermute(x, axis, pairs)  6.42 us
    another operation x14, other arithmetic  4.75 us
    dot_general x1, matrix products, body(): jnp.einsum('tfk,tkv->fv', binned, lax.all_gather(tables, 'det', axis=2, t...  4.07 us
  transfers between devices with their start and end apart: 14, of which 4 were waited for; matrix products, arithmetic and copies ran while one was open for 8% of the time, Pallas kernels for 0%

commit v1 on v0

--- a/solution.py
+++ b/solution.py
@@ -6,6 +6,11 @@
 KWIN = 256
 NTAB = 4
 RANGE = 3
+
+
+def swapped_in(block, mesh_axis, along):
+    repeated = jnp.stack([block] * lax.axis_size(mesh_axis))
+    return jnp.concatenate(lax.all_to_all(repeated, mesh_axis, 0, 0), axis=along)
 
 
 def shifted(x, axis, by):
@@ -47,10 +52,7 @@
         stacked = stacked + bin_windows(arrived_windows, arrived_slots, everything)
     binned = stacked.astype(jnp.bfloat16)
     partial_image = jnp.einsum(
-        "tfk,tkv->fv",
-        binned,
-        lax.all_gather(tables, "det", axis=2, tiled=True),
-        preferred_element_type=jnp.float32,
+        "tfk,tkv->fv", binned, swapped_in(tables, "det", 2), preferred_element_type=jnp.float32
     )
     return lax.psum_scatter(partial_image, "det", scatter_dimension=1, tiled=True)
 

time: 130 us -> 149 us (1.15)
  waiting for transfers between devices: 48.5 us -> 67.3 us
  local copies, waits for them, and re-layouts: 4.5 us -> 8.47 us
  matrix products: 4.07 us -> 1.99 us
  other arithmetic: 6.48 us -> 4.87 us
    all_to_all x0 -> x1, waiting for transfers between devices: none -> 25.7 us  [swapped_in(): lax.all_to_all(repeated, mesh_axis, 0, 0)]
    all_gather x1 -> x0, waiting for transfers between devices: 15.4 us -> none  [body(): lax.all_gather(tables, 'det', axis=2, tiled=True)]
    ppermute x12, waiting for transfers between devices: 6.42 us -> 15 us  [shifted(): return lax.ppermute(x, axis, pairs)]
    all_to_all x0 -> x1, starting transfers between devices: none -> 6.48 us  [swapped_in(): lax.all_to_all(repeated, mesh_axis, 0, 0)]
    ppermute x12, starting transfers between devices: 29.8 us -> 23.8 us  [shifted(): return lax.ppermute(x, axis, pairs)]
    another operation x0 -> x1, local copies, waits for them, and re-layouts: none -> 3.65 us  [swapped_in(): repeated = jnp.stack([block] * lax.axis_size(mesh_axis))]
    reshape x0 -> x1, local copies, waits for them, and re-layouts: none -> 2.82 us  [swapped_in(): jnp.concatenate(lax.all_to_all(repeated, mesh_axis, 0, 0), axis=along)]
    dot_general x1, matrix products: 4.07 us -> 1.99 us  [body(): jnp.einsum('tfk,tkv->fv', binned, swapped_in(tables, 'det', 2), preferred...]
  transfers between devices with their start and end apart: 14 -> 14, of which waited for: 4 -> 7; matrix products, arithmetic and copies ran while one was open for 8% -> 5% of each run, Pallas kernels for 0% -> 0%
where the time goes in v1:
time: 149 us; the launch traced here: 148 us
  waiting for transfers between devices  67.3 us (45%)
  between operations  35.5 us (24%)
  starting transfers between devices  30.2 us (20%)
  local copies, waits for them, and re-layouts  8.47 us (6%)
  other arithmetic  4.87 us (3%)
  matrix products  1.99 us (1%)
    reduce_scatter x1, waiting for transfers between devices, body(): lax.psum_scatter(partial_image, 'det', scatter_dimension=1, tiled=True)  26.6 us
    all_to_all x1, waiting for transfers between devices, swapped_in(): lax.all_to_all(repeated, mesh_axis, 0, 0)  25.7 us
    ppermute x12, starting transfers between devices, shifted(): return lax.ppermute(x, axis, pairs)  23.8 us
    ppermute x12, waiting for transfers between devices, shifted(): return lax.ppermute(x, axis, pairs)  15 us
    all_to_all x1, starting transfers between devices, swapped_in(): lax.all_to_all(repeated, mesh_axis, 0, 0)  6.48 us
    another operation x14, other arithmetic  4.75 us
    another operation x1, local copies, waits for them, and re-layouts, swapped_in(): repeated = jnp.stack([block] * lax.axis_size(mesh_axis))  3.65 us
  transfers between devices with their start and end apart: 14, of which 7 were waited for; matrix products, arithmetic and copies ran while one was open for 5% of the time, Pallas kernels for 0%

profile of v1, /device:TPU:0, one launch (start us, length us, event | category | flops | bytes accessed | tf_op | source)
XLA Modules:
  0.0 148.4 jit_solution(17847689670811492156)
XLA Ops:
  6.5 3.7 %stack.2 = bf16[4,4,256,512]{3,2,1,0:T(8,128)(2,1)} broadcast(bf16[4,256,512]{2,1,0:T(8,128)(2,1)} %param.6), dimensions={1,2,3} | broadcast | bytes 5242880 | tf_op jit(solution)/shard_map/stack | solution.py:12
  10.2 6.5 %all-to-all-start = ((bf16[4,4,256,512]{3,2,1,0:T(8,128)(2,1)}), bf16[4,4,256,512]{3,2,1,0:T(8,128)(2,1)}, u32[]{:S(2)}, u32[]{:S(2)}) async-start(bf16[4,4,256,512]{3,2,1,0:T(8,128)(2,1)} %stack.2), calls=%async_computation | async-start | bytes 8388608 | tf_op jit(solution)/shard_map/all_to_all | solution.py:13
  16.7 0.0 reduce-scatter.2.cloned.1.call-start
  16.7 0.0 copy-done.1
  16.7 0.7 fusion.22
  19.8 0.0 copy-done.3
  19.8 0.6 fusion.23
  34.1 0.0 copy-done
  34.1 0.1 convert_element_type.10
  38.8 0.2 bitcast_convert_fusion.6
  39.0 2.9 %collective-permute-start.11 = (bf16[1,128,256]{2,1,0:T(8,128)(2,1)S(1)}, bf16[1,128,256]{2,1,0:T(8,128)(2,1)S(1)}, u32[]{:S(2)}, u32[]{:S(2)}) collective-permute-start(bf16[1,128,256]{2,1,0:T(8,128)(2,1)S(1)} %get-tuple-element.83), channel_id=1, source_target_pairs={{0,12},{4,16},{8,20},{12,24},{16,28},{1,13},{5,17},{9,21},{13,25},... | collective-permute-start | bytes 196616 | tf_op jit(solution)/shard_map/ppermute | solution.py:19
  41.9 0.0 copy-done.2
  42.0 0.7 fusion.21
  42.6 4.3 %collective-permute-start.10 = (s32[1]{0:T(128)}, s32[1]{0:T(128)}, u32[]{:S(2)}, u32[]{:S(2)}) collective-permute-start(s32[1]{0:T(128)} %bitcast.49), channel_id=1, source_target_pairs={{0,12},{4,16},{8,20},{12,24},{16,28},{1,13},{5,17},{9,21},{13,25},... | collective-permute-start | bytes 20 | tf_op jit(solution)/shard_map/ppermute | solution.py:19
  46.9 1.3 collective-permute-start.9
  48.2 3.7 %collective-permute-start.8 = (s32[1]{0:T(128)}, s32[1]{0:T(128)}, u32[]{:S(2)}, u32[]{:S(2)}) collective-permute-start(s32[1]{0:T(128)} %bitcast.41), channel_id=1, source_target_pairs={{0,8},{4,12},{8,16},{12,20},{16,24},{20,28},{1,9},{5,13},{9,17},{1... | collective-permute-start | bytes 20 | tf_op jit(solution)/shard_map/ppermute | solution.py:19
  51.9 1.3 collective-permute-start.7
  54.4 0.7 fusion.14
  55.0 0.0 collective-permute-done.10
  55.1 2.6 %collective-permute-start.6 = (s32[1]{0:T(128)}, s32[1]{0:T(128)}, u32[]{:S(2)}, u32[]{:S(2)}) collective-permute-start(s32[1]{0:T(128)} %bitcast.33), channel_id=1, source_target_pairs={{0,4},{4,8},{8,12},{12,16},{16,20},{20,24},{24,28},{1,5},{5,9},{9,... | collective-permute-start | bytes 20 | tf_op jit(solution)/shard_map/ppermute | solution.py:19
  57.7 0.6 fusion.20
  58.3 0.0 collective-permute-done.8
  58.3 1.3 collective-permute-start.5
  59.6 0.6 fusion.19
  60.3 0.0 collective-permute-done.6
  60.3 1.3 collective-permute-start.4
  61.6 0.6 fusion.18
  62.1 2.0 %collective-permute-done.4 = s32[1]{0:T(128)} collective-permute-done((s32[1]{0:T(128)}, s32[1]{0:T(128)}, u32[]{:S(2)}, u32[]{:S(2)}) %collective-permute-start.4) | collective-permute-done | bytes 36 | tf_op jit(solution)/shard_map/ppermute | solution.py:19
  64.1 1.3 collective-permute-start.2
  65.4 0.6 fusion.17
  66.1 3.6 %collective-permute-done.2 = s32[1]{0:T(128)} collective-permute-done((s32[1]{0:T(128)}, s32[1]{0:T(128)}, u32[]{:S(2)}, u32[]{:S(2)}) %collective-permute-start.2) | collective-permute-done | bytes 36 | tf_op jit(solution)/shard_map/ppermute | solution.py:19
  69.7 1.3 collective-permute-start
  71.0 0.6 fusion.16
  71.7 3.8 %collective-permute-done = s32[1]{0:T(128)} collective-permute-done((s32[1]{0:T(128)}, s32[1]{0:T(128)}, u32[]{:S(2)}, u32[]{:S(2)}) %collective-permute-start) | collective-permute-done | bytes 36 | tf_op jit(solution)/shard_map/ppermute | solution.py:19
  75.5 1.3 collective-permute-start.3
  76.8 0.7 fusion.15
  77.5 0.0 collective-permute-done.11
  77.5 1.3 collective-permute-start.1
  78.8 0.0 collective-permute-done.9
  78.8 0.0 collective-permute-done.7
  78.8 0.0 collective-permute-done.5
  78.9 3.8 %collective-permute-done.3 = bf16[1,128,256]{2,1,0:T(8,128)(2,1)S(1)} collective-permute-done((bf16[1,128,256]{2,1,0:T(8,128)(2,1)S(1)}, bf16[1,128,256]{2,1,0:T(8,128)(2,1)S(1)}, u32[]{:S(2)}, u32[]{:S(2)}) %collective-permute-start.3) | collective-permute-done | bytes 65568 | tf_op jit(solution)/shard_map/ppermute | solution.py:19
  82.7 1.6 %collective-permute-done.1 = bf16[1,128,256]{2,1,0:T(8,128)(2,1)S(1)} collective-permute-done((bf16[1,128,256]{2,1,0:T(8,128)(2,1)S(1)}, bf16[1,128,256]{2,1,0:T(8,128)(2,1)S(1)}, u32[]{:S(2)}, u32[]{:S(2)}) %collective-permute-start.1) | collective-permute-done | bytes 65568 | tf_op jit(solution)/shard_map/ppermute | solution.py:19
  84.4 25.7 %all-to-all-done = bf16[4,4,256,512]{3,2,1,0:T(8,128)(2,1)} async-done(((bf16[4,4,256,512]{3,2,1,0:T(8,128)(2,1)}), bf16[4,4,256,512]{3,2,1,0:T(8,128)(2,1)}, u32[]{:S(2)}, u32[]{:S(2)}) %all-to-all-start) | async-done | bytes 4194336 | tf_op jit(solution)/shard_map/all_to_all | solution.py:13
  110.1 2.8 %copy.7 = bf16[4,4,32,8,512]{4,3,0,2,1:T(8,128)(2,1)S(1)} copy(bf16[4,4,32,8,512]{4,3,2,1,0:T(8,128)(2,1)} %bitcast.66) | data formatting | bytes 8388608 | tf_op jit(solution)/shard_map/reshape | solution.py:13
  112.9 2.0 %convolution_bitcast_fusion = f32[128,2048]{1,0:T(8,128)} fusion(bf16[4,256,2048]{2,1,0:T(8,128)(2,1)S(1)} %bitcast.84, f32[128,256]{1,0:T(8,128)S(1)} %bitcast_convert_fusion, f32[4]{0:T(128)S(1)} %fusion.20, f32[128,256]{1,0:T(8,128)S(1)} %bitcast_convert_fusion.1, f32[4]{0:T(128)S(1)} %fusion.19, f32[128,256]{1,0:T(8,128)S(1)} %bitcast_convert_fusion.2, ...), kind=kOutput, calls=%fused_computation | convolution fusion | flops 538705920 | bytes 6160496 | tf_op jit(solution)/shard_map/tfk,tkv->fv/dot_general | solution.py:54
  114.9 0.0 reduce-scatter.2.cloned.1.call-update
  114.9 26.6 %reduce-scatter.2.cloned.1.call-done = f32[128,512]{1,0:T(8,128)} async-done(((f32[128,2048]{1,0:T(8,128)}), f32[128,512]{1,0:T(8,128)}) %reduce-scatter.2.cloned.1.call-update) | async-done | bytes 262160 | tf_op jit(solution)/shard_map/reduce_scatter | solution.py:57
  (10 shorter events, 0.1 us)
Async XLA Ops:
  10.2 6.5 %copy-start.1 = (s32[1,7]{1,0:T(1,128)S(1)}, s32[1,7]{1,0:T(1,128)}, u32[]{:S(2)}) copy-start(s32[1,7]{1,0:T(1,128)} %param.9) | copy-start | bytes 88
  10.2 9.6 %copy-start.3 = (s32[1,2]{1,0:T(1,128)S(1)}, s32[1,2]{1,0:T(1,128)}, u32[]{:S(2)}) copy-start(s32[1,2]{1,0:T(1,128)} %param.7) | copy-start | bytes 28
  10.2 23.9 %copy-start = (f32[1,128,4096]{2,1,0:T(8,128)S(1)}, f32[1,128,4096]{2,1,0:T(8,128)}, u32[]{:S(2)}) copy-start(f32[1,128,4096]{2,1,0:T(8,128)} %param.5) | copy-start | bytes 6291460
  10.2 99.9 %all-to-all-start = ((bf16[4,4,256,512]{3,2,1,0:T(8,128)(2,1)}), bf16[4,4,256,512]{3,2,1,0:T(8,128)(2,1)}, u32[]{:S(2)}, u32[]{:S(2)}) async-start(bf16[4,4,256,512]{3,2,1,0:T(8,128)(2,1)} %stack.2), calls=%async_computation | async-start | bytes 8388608 | tf_op jit(solution)/shard_map/all_to_all | solution.py:13
  16.7 25.3 %copy-start.2 = (s32[1,7]{1,0:T(1,128)S(1)}, s32[1,7]{1,0:T(1,128)}, u32[]{:S(2)}) copy-start(s32[1,7]{1,0:T(1,128)} %param.8) | copy-start | bytes 88
  16.7 124.9 %reduce-scatter.2.cloned.1.call-start = ((), (), s32[]{:S(2)}) async-start(), calls=%async_computation.2 | async-start | bytes 1310720 | tf_op jit(solution)/shard_map/reduce_scatter | solution.py:57
  39.0 38.4 %collective-permute-start.11 = (bf16[1,128,256]{2,1,0:T(8,128)(2,1)S(1)}, bf16[1,128,256]{2,1,0:T(8,128)(2,1)S(1)}, u32[]{:S(2)}, u32[]{:S(2)}) collective-permute-start(bf16[1,128,256]{2,1,0:T(8,128)(2,1)S(1)} %get-tuple-element.83), channel_id=1, source_target_pairs={{0,12},{4,16},{8,20},{12,24},{16,28},{1,13},{5,17},{9,21},{13,25},... | collective-permute-start | bytes 196616 | tf_op jit(solution)/shard_map/ppermute | solution.py:19
  42.6 12.4 %collective-permute-start.10 = (s32[1]{0:T(128)}, s32[1]{0:T(128)}, u32[]{:S(2)}, u32[]{:S(2)}) collective-permute-start(s32[1]{0:T(128)} %bitcast.49), channel_id=1, source_target_pairs={{0,12},{4,16},{8,20},{12,24},{16,28},{1,13},{5,17},{9,21},{13,25},... | collective-permute-start | bytes 20 | tf_op jit(solution)/shard_map/ppermute | solution.py:19
  46.9 31.9 %collective-permute-start.9 = (bf16[1,128,256]{2,1,0:T(8,128)(2,1)S(1)}, bf16[1,128,256]{2,1,0:T(8,128)(2,1)S(1)}, u32[]{:S(2)}, u32[]{:S(2)}) collective-permute-start(bf16[1,128,256]{2,1,0:T(8,128)(2,1)S(1)} %get-tuple-element.84), channel_id=1, source_target_pairs={{0,8},{4,12},{8,16},{12,20},{16,24},{20,28},{1,9},{5,13},{9,17},{1... | collective-permute-start | bytes 196616 | tf_op jit(solution)/shard_map/ppermute | solution.py:19
  48.2 10.1 %collective-permute-start.8 = (s32[1]{0:T(128)}, s32[1]{0:T(128)}, u32[]{:S(2)}, u32[]{:S(2)}) collective-permute-start(s32[1]{0:T(128)} %bitcast.41), channel_id=1, source_target_pairs={{0,8},{4,12},{8,16},{12,20},{16,24},{20,28},{1,9},{5,13},{9,17},{1... | collective-permute-start | bytes 20 | tf_op jit(solution)/shard_map/ppermute | solution.py:19
  51.9 26.9 %collective-permute-start.7 = (bf16[1,128,256]{2,1,0:T(8,128)(2,1)S(1)}, bf16[1,128,256]{2,1,0:T(8,128)(2,1)S(1)}, u32[]{:S(2)}, u32[]{:S(2)}) collective-permute-start(bf16[1,128,256]{2,1,0:T(8,128)(2,1)S(1)} %get-tuple-element.85), channel_id=1, source_target_pairs={{0,4},{4,8},{8,12},{12,16},{16,20},{20,24},{24,28},{1,5},{5,9},{9,... | collective-permute-start | bytes 196616 | tf_op jit(solution)/shard_map/ppermute | solution.py:19
  55.1 5.2 %collective-permute-start.6 = (s32[1]{0:T(128)}, s32[1]{0:T(128)}, u32[]{:S(2)}, u32[]{:S(2)}) collective-permute-start(s32[1]{0:T(128)} %bitcast.33), channel_id=1, source_target_pairs={{0,4},{4,8},{8,12},{12,16},{16,20},{20,24},{24,28},{1,5},{5,9},{9,... | collective-permute-start | bytes 20 | tf_op jit(solution)/shard_map/ppermute | solution.py:19
  58.3 20.5 %collective-permute-start.5 = (bf16[1,128,256]{2,1,0:T(8,128)(2,1)S(1)}, bf16[1,128,256]{2,1,0:T(8,128)(2,1)S(1)}, u32[]{:S(2)}, u32[]{:S(2)}) collective-permute-start(bf16[1,128,256]{2,1,0:T(8,128)(2,1)S(1)} %get-tuple-element.86), channel_id=1, source_target_pairs={{4,0},{8,4},{12,8},{16,12},{20,16},{24,20},{28,24},{5,1},{9,5},{13... | collective-permute-start | bytes 196616 | tf_op jit(solution)/shard_map/ppermute | solution.py:19
  60.3 3.9 %collective-permute-start.4 = (s32[1]{0:T(128)}, s32[1]{0:T(128)}, u32[]{:S(2)}, u32[]{:S(2)}) collective-permute-start(s32[1]{0:T(128)} %bitcast.25), channel_id=1, source_target_pairs={{4,0},{8,4},{12,8},{16,12},{20,16},{24,20},{28,24},{5,1},{9,5},{13... | collective-permute-start | bytes 20 | tf_op jit(solution)/shard_map/ppermute | solution.py:19
  64.1 5.6 %collective-permute-start.2 = (s32[1]{0:T(128)}, s32[1]{0:T(128)}, u32[]{:S(2)}, u32[]{:S(2)}) collective-permute-start(s32[1]{0:T(128)} %bitcast.17), channel_id=1, source_target_pairs={{8,0},{12,4},{16,8},{20,12},{24,16},{28,20},{9,1},{13,5},{17,9},{2... | collective-permute-start | bytes 20 | tf_op jit(solution)/shard_map/ppermute | solution.py:19
  69.7 5.7 %collective-permute-start = (s32[1]{0:T(128)}, s32[1]{0:T(128)}, u32[]{:S(2)}, u32[]{:S(2)}) collective-permute-start(s32[1]{0:T(128)} %bitcast.9), channel_id=1, source_target_pairs={{12,0},{16,4},{20,8},{24,12},{28,16},{13,1},{17,5},{21,9},{25,13},... | collective-permute-start | bytes 20 | tf_op jit(solution)/shard_map/ppermute | solution.py:19
  75.5 7.2 %collective-permute-start.3 = (bf16[1,128,256]{2,1,0:T(8,128)(2,1)S(1)}, bf16[1,128,256]{2,1,0:T(8,128)(2,1)S(1)}, u32[]{:S(2)}, u32[]{:S(2)}) collective-permute-start(bf16[1,128,256]{2,1,0:T(8,128)(2,1)S(1)} %get-tuple-element.87), channel_id=1, source_target_pairs={{8,0},{12,4},{16,8},{20,12},{24,16},{28,20},{9,1},{13,5},{17,9},{2... | collective-permute-start | bytes 196616 | tf_op jit(solution)/shard_map/ppermute | solution.py:19
  77.5 6.9 %collective-permute-start.1 = (bf16[1,128,256]{2,1,0:T(8,128)(2,1)S(1)}, bf16[1,128,256]{2,1,0:T(8,128)(2,1)S(1)}, u32[]{:S(2)}, u32[]{:S(2)}) collective-permute-start(bf16[1,128,256]{2,1,0:T(8,128)(2,1)S(1)} %get-tuple-element.88), channel_id=1, source_target_pairs={{12,0},{16,4},{20,8},{24,12},{28,16},{13,1},{17,5},{21,9},{25,13},... | collective-permute-start | bytes 196616 | tf_op jit(solution)/shard_map/ppermute | solution.py:19
Sparse Core Ops, SparseCore 0:
  115.1 26.4 reduce-scatter.1
